TPU v7x, 8 devices: a whole 2x2x1 slice. The times are simulated.
8 devices in a mesh: rep: 1 (over z), tp: 2 (over y), dp: 4 (over x, core).
Axes of the slice: x: 2, y: 2, z: 1, core: 2. Of those that a mesh axis runs over, the one named last changes fastest.
Arguments:
- grad_partial: float32 [4, 24, 2048, 768], P(('rep', 'dp'), None, None, 'tp')
- momentum: float32 [24, 2048, 768], P('rep', 'dp', 'tp')
- weight: float32 [24, 2048, 768], P('rep', 'dp', 'tp')
- learn_rate: float32 [24], P('rep')
- decay_rate: float32 [], replicated
Outputs:
- output 1: float32 [24, 2048, 768], P('rep', 'dp', 'tp')
- output 2: float32 [24, 2048, 768], P('rep', 'dp', 'tp')
- output 3: bfloat16 [24, 2048, 768], P('rep', None, 'tp')
All inputs are finite; a program needn't handle non-finite values.
Results may differ from a plain program's by a relative error of at most 0.0130496.
Values are sent between devices in bfloat16 or wider.
A program may use at most 1 GiB of HBM per device.

v0:
```python
import functools
import math

import jax
import jax.numpy as jnp
from jax import lax
from jax.experimental import pallas as pl
from jax.experimental.pallas import tpu as pltpu
from jax.sharding import PartitionSpec as P


MOMENTUM = 0.95
NS_STEPS = 5
COEF_A = 3.4445
COEF_B = -4.7750
COEF_C = 2.0315
NORM_EPS = 1e-7

MESH = pl.DeviceIdType.MESH
F32 = jnp.float32
BF16 = jnp.bfloat16

MATS = 24
ROWS = 2048
COLS = 768
DEVS = 8
ROUNDS = MATS // DEVS
RB = ROWS // 4
CB = COLS // 2
OUT_SCALE = 0.2 * math.sqrt(max(ROWS, COLS))

LAG = 3
LEAD = 2
A_SLOTS = 2 * LEAD
B_SLOTS = 2 * LAG
NS_START = (8 + LAG + 2, 16 + LAG + 2, 24 + LAG)
W_START = (NS_START[0] + 7, NS_START[2])
STEPS = NS_START[2] + NS_STEPS
CHUNK = 64
HEAD = MATS - DEVS
TAILS = ((0, 1, 0, RB), (1, 4, 0, RB), (5, 2, 0, RB), (7, 1, 0, RB // 2), (7, 1, RB // 2, RB // 2))
PIECES = 4
PIECE = RB // PIECES


def rem(a, b):
    return lax.rem(a, b)


def owner_of(yy, dd):
    return yy * 4 + rem(dd, 2) * 2 + lax.div(dd, 2)


def shifted(yy, dd, i):
    dx, dy, dc = lax.div(i, 4), rem(lax.div(i, 2), 2), rem(i, 2)
    xx = rem(lax.div(dd, 2) + dx, 2)
    return rem(yy + dy, 2), xx * 2 + rem(rem(dd, 2) + dc, 2)


def row_loop(total, body):
    @pl.loop(0, total // CHUNK)
    def _(i):
        body(pl.ds(pl.multiple_of(i * CHUNK, CHUNK), CHUNK))


def kernel(
    grad, mom, wt, rate_in, decay,
    mom_o, wt_o, wb_o, tail_0, tail_1, tail_2, tail_3, tail_4, mid,
    rate, rate_sem, own, ra, sendb, recvb, acc, momi, momq, wti, wtq, ust, wst, xb, rx, gram, poly,
    mid_recv, p_send, p_recv, own_sem, a_send, a_recv, rs_send, rs_recv, momi_sem, momq_sem, wti_sem, wtq_sem,
    u_send, u_recv, x_send, x_recv, w_loc, w_par, w_nbr, wp_recv, wx_recv, f_send, f_recv,
):
    dp = lax.axis_index("dp")
    y = lax.axis_index("tp")
    x = lax.div(dp, 2)
    c = rem(dp, 2)
    me = owner_of(y, dp)
    partner = {"tp": y, "dp": x * 2 + (1 - c)}
    nbr_dp = (1 - x) * 2 + c
    nbr = {"tp": y, "dp": nbr_dp}

    def coords(i):
        return shifted(y, dp, i)

    def remote(src, dst, ss, rs, dev):
        return pltpu.make_async_remote_copy(
            src_ref=src, dst_ref=dst, send_sem=ss, recv_sem=rs, device_id=dev, device_id_type=MESH
        )

    def xblock(r, dd, yy):
        return xb.at[
            r, pl.ds(pl.multiple_of(dd * RB, RB), RB), pl.ds(pl.multiple_of(yy * CB, CB), CB)
        ]

    def rate_copy():
        return pltpu.make_async_copy(rate_in, rate, rate_sem.at[0])

    def own_copy(t):
        s = rem(t, 2)
        return pltpu.make_async_copy(grad.at[t, :, c], own.at[s], own_sem.at[s])

    def a_copy(t):
        s = rem(t, A_SLOTS)
        return remote(grad.at[t, :, 1 - c], ra.at[s], a_send.at[s], a_recv.at[s], partner)

    def rs_copy(t):
        s, d = rem(t, LAG), rem(t, B_SLOTS)
        return remote(sendb.at[s], recvb.at[d], rs_send.at[s], rs_recv.at[d], nbr)

    def mom_load(j):
        s = rem(j, 2)
        return pltpu.make_async_copy(mom.at[j], momi.at[s], momi_sem.at[s])

    def mom_store(j):
        s = rem(j, 2)
        return pltpu.make_async_copy(momq.at[s], mom_o.at[j], momq_sem.at[s])

    def u_copy(j):
        k = rem(j, DEVS)
        r = lax.div(j, DEVS)
        dev = {"tp": lax.div(k, 4), "dp": rem(k, 2) * 2 + rem(lax.div(k, 2), 2)}
        return remote(ust.at[k], xblock(r, dp, y), u_send.at[k], u_recv.at[r * DEVS + me], dev)

    def x_copy(r, i):
        yy, dd = coords(i)
        j = r * DEVS + me
        return remote(
            xblock(r, dd, yy), rx.at[j], x_send.at[r * DEVS + i], x_recv.at[j], {"tp": yy, "dp": dd}
        )

    def w_mat(w):
        return lax.div(w, DEVS) * DEVS + owner_of(*coords(rem(w, DEVS)))

    def wt_load(w):
        s = rem(w, 2)
        return pltpu.make_async_copy(wt.at[w_mat(w)], wti.at[s], wti_sem.at[s])

    def wt_store(w):
        s = rem(w, 2)
        return pltpu.make_async_copy(wtq.at[s], wt_o.at[w_mat(w)], wtq_sem.at[s])

    def w_copies(w):
        j, s = w_mat(w), rem(w, DEVS)
        dst = wb_o.at[j, dp]
        return (
            pltpu.make_async_copy(wst.at[s], dst, w_loc.at[s]),
            remote(wst.at[s], dst, w_par.at[s], wp_recv.at[j], partner),
            remote(wst.at[s], dst, w_nbr.at[s], wx_recv.at[j], nbr),
        )

    def tail_copies(w):
        s = rem(w, DEVS)
        for ref, (first, count, row, rows) in zip((tail_0, tail_1, tail_2, tail_3, tail_4), TAILS):
            low = HEAD + first
            yield low, low + count, lambda ref=ref, low=low, row=row, rows=rows: pltpu.make_async_copy(
                wst.at[s, pl.ds(row, rows), :], ref.at[w - low], w_loc.at[s]
            )

    def mid_copy():
        return remote(wst.at[0], mid.at[0], w_nbr.at[0], mid_recv.at[0], nbr)

    def f_mat(w):
        return lax.div(w, DEVS) * DEVS + owner_of(*shifted(y, nbr_dp, rem(w, DEVS)))

    def f_copy(w):
        j = f_mat(w)
        ref = wb_o.at[j, nbr_dp]
        return remote(ref, ref, f_send.at[j], f_recv.at[j], partner)

    def presum(t):
        own_copy(t).wait()
        a_copy(t).wait_recv()

        @pl.when(t >= LAG)
        def _():
            rs_copy(t - LAG).wait_send()

        so, sa, ss = rem(t, 2), rem(t, A_SLOTS), rem(t, LAG)

        def body(rows):
            sendb[ss, rows, :] = own[so, 1 - x, rows, :] + ra[sa, 1 - x, rows, :]
            acc[ss, rows, :] = own[so, x, rows, :] + ra[sa, x, rows, :]

        row_loop(RB, body)
        rs_copy(t).start()

        @pl.when(t + 2 < MATS)
        def _():
            own_copy(t + 2).start()

        @pl.when(t + LEAD < MATS)
        def _():
            @pl.when(t + LEAD > A_SLOTS)
            def _():
                a_copy(t + LEAD - A_SLOTS).wait_send()

            a_copy(t + LEAD).start()

    def piece_copy(q):
        if q == PIECES:
            src, dst = grad.at[0, x, 1 - c], ra.at[0, x]
        else:
            rows = pl.ds(q * PIECE, PIECE)
            src, dst = wtq.at[0, rows, :], ra.at[0, 1 - x, rows, :]
        return remote(src, dst, p_send.at[q], p_recv.at[q], partner)

    def stage_copy():
        return pltpu.make_async_copy(grad.at[0, 1 - x, 1 - c], wtq.at[0], wtq_sem.at[0])

    def presum_first():
        own_copy(0).wait()
        for q in range(PIECES):
            piece_copy(q).wait_recv()
            rows = pl.ds(q * PIECE, PIECE)
            sendb[0, rows, :] = own[0, 1 - x, rows, :] + ra[0, 1 - x, rows, :]
            remote(
                sendb.at[0, rows, :], recvb.at[0, rows, :], rs_send.at[0], rs_recv.at[0], nbr
            ).start()
        piece_copy(PIECES).wait_recv()

        def body(rows):
            acc[0, rows, :] = own[0, x, rows, :] + ra[0, x, rows, :]

        row_loop(RB, body)
        own_copy(2).start()
        a_copy(LEAD).start()
        for q in range(PIECES + 1):
            piece_copy(q).wait_send()

    def finish(j):
        mom_load(j).wait()

        @pl.when(j >= 2)
        def _():
            mom_store(j - 2).wait()

        k = rem(j, DEVS)
        r = lax.div(j, DEVS)

        @pl.when((j >= DEVS) & (k != me))
        def _():
            u_copy(j - DEVS).wait_send()

        rs_copy(j).wait_recv()
        sm, ss, sr = rem(j, 2), rem(j, LAG), rem(j, B_SLOTS)

        def body(rows):
            mean = (acc[ss, rows, :] + recvb[sr, rows, :]) * 0.25
            new = MOMENTUM * momi[sm, rows, :] + mean
            momq[sm, rows, :] = new
            ust[k, rows, :] = (mean + MOMENTUM * new).astype(BF16)

        row_loop(RB, body)

        @pl.when(k != me)
        def _():
            u_copy(j).start()

        mom_store(j).start()

        @pl.when(j + 2 < MATS)
        def _():
            mom_load(j + 2).start()

        for half in range(2):
            @pl.when((k == me) & (y == half))
            def _():
                def put(rows):
                    dst = pl.ds(pl.multiple_of(dp * RB + rows.start, CHUNK), CHUNK)
                    xb[r, dst, half * CB:(half + 1) * CB] = ust[k, rows, :]

                row_loop(RB, put)

    def normalize(r):
        def square(i, total):
            v = xb[r, pl.ds(pl.multiple_of(i * CHUNK, CHUNK), CHUNK), :].astype(F32)
            return total + jnp.sum((v * v).reshape(CHUNK // 8, 8, COLS), axis=0)

        total = lax.fori_loop(0, ROWS // CHUNK, square, jnp.zeros((8, COLS), F32))
        norm = jnp.sqrt(jnp.sum(total, keepdims=True)) + NORM_EPS

        def scale(rows):
            xb[r, rows, :] = (xb[r, rows, :].astype(F32) / norm).astype(BF16)

        row_loop(ROWS, scale)

    def iterate(r):
        @pl.loop(0, COLS // 256)
        def _(m):
            cols = pl.ds(pl.multiple_of(m * 256, 256), 256)
            gram[cols, :] = lax.dot_general(
                xb[r, :, cols], xb[r], (((0,), (0,)), ((), ())), preferred_element_type=F32
            ).astype(BF16)

        @pl.loop(0, COLS // 256)
        def _(m):
            rows = pl.ds(pl.multiple_of(m * 256, 256), 256)
            part = gram[rows, :]
            square = jnp.dot(part, gram[...], preferred_element_type=F32)
            poly[rows, :] = (COEF_B * part.astype(F32) + COEF_C * square).astype(BF16)

        @pl.loop(0, ROWS // 512)
        def _(m):
            rows = pl.ds(pl.multiple_of(m * 512, 512), 512)
            part = xb[r, rows, :]
            prod = jnp.dot(part, poly[...], preferred_element_type=F32)
            xb[r, rows, :] = (COEF_A * part.astype(F32) + prod).astype(BF16)

    def ortho(r, s):
        @pl.when(s == 0)
        def _():
            @pl.loop(1, DEVS)
            def _(i):
                yy, dd = coords(i)
                remote(
                    ust.at[0], xblock(r, dd, yy), u_send.at[0],
                    u_recv.at[r * DEVS + owner_of(yy, dd)], partner,
                ).wait_recv()

            normalize(r)

        iterate(r)

        @pl.when(s == NS_STEPS - 1)
        def _():
            @pl.loop(0, DEVS)
            def _(n):
                i = rem(n + 4, DEVS)

                @pl.when(i != 0)
                def _():
                    x_copy(r, i).start()

            for half in range(2):
                @pl.when(y == half)
                def _():
                    def put(rows):
                        src = pl.ds(pl.multiple_of(dp * RB + rows.start, CHUNK), CHUNK)
                        rx[r * DEVS + me, rows, :] = xb[r, src, half * CB:(half + 1) * CB]

                    row_loop(RB, put)

    def forward(w):
        f_copy_in = remote(
            wst.at[0], wb_o.at[f_mat(w), nbr_dp], w_nbr.at[0], wx_recv.at[f_mat(w)], nbr
        )
        f_copy_in.wait_recv()
        f_copy(w).start()

    def weights(w):
        j = w_mat(w)

        @pl.when(rem(w, DEVS) != 0)
        def _():
            remote(xblock(0, 0, 0), rx.at[j], x_send.at[0], x_recv.at[j], nbr).wait_recv()

        wt_load(w).wait()

        @pl.when(w >= 2)
        def _():
            wt_store(w - 2).wait()

        @pl.when(w >= DEVS)
        def _():
            old = w_copies(w - DEVS)
            old[0].wait()
            old[1].wait_send()
            old[2].wait_send()

        s2, s8 = rem(w, 2), rem(w, DEVS)
        lr = rate[j]
        wd = decay[...]

        def body(rows):
            cur = wti[s2, rows, :]
            new = cur - lr * (OUT_SCALE * rx[j, rows, :].astype(F32) + wd * cur)
            wtq[s2, rows, :] = new
            wst[s8, rows, :] = new.astype(BF16)

        row_loop(RB, body)

        @pl.when(w < HEAD)
        def _():
            now = w_copies(w)
            now[2].start()
            now[1].start()
            now[0].start()

        for low, high, copy in tail_copies(w):
            @pl.when((w >= low) & (w < high))
            def _():
                copy().start()

        @pl.when(w == HEAD)
        def _():
            mid_copy().start()

        wt_store(w).start()

        @pl.when(w + 2 < MATS)
        def _():
            wt_load(w + 2).start()

        @pl.when((w >= DEVS) & (w < HEAD))
        def _():
            forward(w - DEVS)

    barrier = pltpu.get_barrier_semaphore()
    for i in range(1, DEVS):
        yy, dd = coords(i)
        pl.semaphore_signal(barrier, inc=1, device_id={"tp": yy, "dp": dd}, device_id_type=MESH)
    stage_copy().start()
    own_copy(0).start()
    pl.semaphore_wait(barrier, DEVS - 1)

    stage_copy().wait()
    for q in range(PIECES + 1):
        piece_copy(q).start()
    for t in range(1, LEAD):
        a_copy(t).start()
    own_copy(1).start()
    rate_copy().start()
    for t in range(2):
        mom_load(t).start()
        wt_load(t).start()
    presum_first()
    rate_copy().wait()

    def w_done(t):
        return (
            jnp.minimum(4 * jnp.clip(t - W_START[0], 0, 1) + 2 * jnp.clip(t - W_START[0] - 1, 0, 2), 8)
            + jnp.minimum(4 * jnp.clip(t - W_START[1], 0, 1) + 2 * jnp.clip(t - W_START[1] - 1, 0, 2), 8)
        )

    @pl.loop(0, STEPS)
    def _(t):
        @pl.when((t >= LAG) & (t < MATS + LAG))
        def _():
            finish(t - LAG)

        @pl.when((t >= 1) & (t < MATS))
        def _():
            presum(t)

        pl.loop(w_done(t), w_done(t + 1))(weights)

        r = jnp.where(t >= NS_START[2], 2, jnp.where(t >= NS_START[1], 1, 0))
        base = jnp.where(
            t >= NS_START[2], NS_START[2], jnp.where(t >= NS_START[1], NS_START[1], NS_START[0])
        )

        @pl.when((t >= base) & (t < base + NS_STEPS))
        def _():
            ortho(r, t - base)

    @pl.loop(HEAD - DEVS, HEAD)
    def _(w):
        forward(w)

    for t in range(MATS - LAG, MATS):
        rs_copy(t).wait_send()
    for t in range(MATS - A_SLOTS, MATS):
        a_copy(t).wait_send()
    for j in range(MATS - 2, MATS):
        mom_store(j).wait()

    @pl.loop(HEAD, MATS)
    def _(j):
        @pl.when(rem(j, DEVS) != me)
        def _():
            u_copy(j).wait_send()

    def drain_x(r):
        @pl.loop(1, DEVS)
        def _(i):
            x_copy(r, i).wait_send()

    pl.loop(0, ROUNDS - 1)(drain_x)

    @pl.loop(0, HEAD)
    def _(w):
        j = w_mat(w)
        remote(wst.at[0], wb_o.at[j, dp], w_par.at[0], wp_recv.at[j], partner).wait_recv()
        f_copy(w).wait_send()
        ref = wb_o.at[j, 3 - dp]
        remote(ref, ref, f_send.at[j], f_recv.at[j], partner).wait_recv()

    pl.loop(HEAD, MATS)(weights)
    drain_x(ROUNDS - 1)
    for w in range(HEAD, MATS):
        pltpu.make_async_copy(wst.at[0], tail_0.at[0], w_loc.at[w % DEVS]).wait()
    for w in range(MATS - 2, MATS):
        wt_store(w).wait()
    mid_copy().wait()


def publish_kernel(mom, wt, wb, mom_o, wt_o, wb_o):
    mom_o[...] = mom[...]
    wt_o[...] = wt[...]
    wb_o[...] = wb[...]


def publish(mom, wt, wb):
    steps = HEAD
    small = pl.BlockSpec((MATS * RB // steps, CB), lambda i: (i, 0))
    large = pl.BlockSpec((ROWS, CB), lambda i: (i, 0))
    return pl.pallas_call(
        publish_kernel,
        name="publish",
        grid=(steps,),
        out_shape=(
            jax.ShapeDtypeStruct((MATS * RB, CB), F32),
            jax.ShapeDtypeStruct((MATS * RB, CB), F32),
            jax.ShapeDtypeStruct((MATS * ROWS, CB), BF16),
        ),
        in_specs=[small, small, large],
        out_specs=[small, small, large],
        cost_estimate=pl.CostEstimate(
            flops=40_000_000_000, bytes_accessed=126_000_000, transcendentals=0
        ),
        compiler_params=pltpu.CompilerParams(vmem_limit_bytes=44 << 20),
    )(mom.reshape(-1, CB), wt.reshape(-1, CB), wb.reshape(-1, CB))


def fill_kernel(tail, own, par, nbr, fwd, whole, out, sems):
    dp = lax.axis_index("dp")
    y = lax.axis_index("tp")
    places = (dp, dp + 1 - 2 * rem(dp, 2), rem(dp + 2, 4), 3 - dp)
    copies = [
        pltpu.make_async_copy(
            ref.at[i],
            out.at[HEAD + owner_of(*shifted(y, place, tail[0] + i)), place, pl.ds(tail[2], tail[3]), :],
            sems.at[n, i],
        )
        for n, (ref, place) in enumerate(zip((own, par, nbr, fwd), places))
        for i in range(own.shape[0])
    ]
    for copy in copies:
        copy.start()
    for copy in copies:
        copy.wait()


def fill(whole, tail, own, par, nbr, fwd):
    count = own.shape[0]
    hbm = pl.BlockSpec(memory_space=pl.ANY)
    return pl.pallas_call(
        functools.partial(fill_kernel, tail),
        name="fill",
        out_shape=jax.ShapeDtypeStruct(whole.shape, whole.dtype),
        in_specs=[pl.BlockSpec(memory_space=pltpu.VMEM)] * 4 + [hbm],
        out_specs=hbm,
        scratch_shapes=[pltpu.SemaphoreType.DMA((4, count))],
        input_output_aliases={4: 0},
        compiler_params=pltpu.CompilerParams(vmem_limit_bytes=10 << 20),
        cost_estimate=pl.CostEstimate(
            flops=count * 1_000_000_000, bytes_accessed=count * 3_200_000, transcendentals=0
        ),
    )(own, par, nbr, fwd, whole)


def solution(mesh):
    def local_step(grad_local, mom_local, weight_local, learn_rate, decay_rate):
        hbm = pl.BlockSpec(memory_space=pl.ANY)
        dma = pltpu.SemaphoreType.DMA
        block = (RB, CB)
        mom_new, weight_new, head, *tails, mid = pl.pallas_call(
            kernel,
            name="muon_step",
            out_shape=(
                jax.ShapeDtypeStruct((MATS,) + block, F32),
                jax.ShapeDtypeStruct((MATS,) + block, F32),
                jax.ShapeDtypeStruct((HEAD, 4) + block, BF16),
            )
            + tuple(jax.ShapeDtypeStruct((n, rows, CB), BF16) for _, n, _, rows in TAILS)
            + (jax.ShapeDtypeStruct((1,) + block, BF16),),
            in_specs=[hbm] * 4 + [pl.BlockSpec(memory_space=pltpu.SMEM)],
            out_specs=[hbm] * (4 + len(TAILS)),
            scratch_shapes=[
                pltpu.SMEM((MATS,), F32),
                dma((1,)),
                pltpu.VMEM((2, 2) + block, F32),
                pltpu.VMEM((A_SLOTS, 2) + block, F32),
                pltpu.VMEM((LAG,) + block, F32),
                pltpu.VMEM((B_SLOTS,) + block, F32),
                pltpu.VMEM((LAG,) + block, F32),
                pltpu.VMEM((2,) + block, F32),
                pltpu.VMEM((2,) + block, F32),
                pltpu.VMEM((2,) + block, F32),
                pltpu.VMEM((2,) + block, F32),
                pltpu.VMEM((DEVS,) + block, BF16),
                pltpu.VMEM((DEVS,) + block, BF16),
                pltpu.VMEM((ROUNDS, ROWS, COLS), BF16),
                pltpu.VMEM((MATS,) + block, BF16),
                pltpu.VMEM((COLS, COLS), BF16),
                pltpu.VMEM((COLS, COLS), BF16),
                dma((1,)), dma((PIECES + 1,)), dma((PIECES + 1,)),
                dma((2,)), dma((A_SLOTS,)), dma((A_SLOTS,)), dma((LAG,)), dma((B_SLOTS,)),
                dma((2,)), dma((2,)), dma((2,)), dma((2,)),
                dma((DEVS,)), dma((MATS,)), dma((MATS,)), dma((MATS,)),
                dma((DEVS,)), dma((DEVS,)), dma((DEVS,)), dma((MATS,)), dma((MATS,)),
                dma((MATS,)), dma((MATS,)),
            ],
            compiler_params=pltpu.CompilerParams(
                collective_id=0, has_side_effects=True, vmem_limit_bytes=67_000_000
            ),
            cost_estimate=pl.CostEstimate(
                flops=3 * 28_700_000_000, bytes_accessed=400_000_000, transcendentals=0
            ),
        )(
            grad_local.reshape((MATS, 2, 2) + block),
            mom_local,
            weight_local,
            learn_rate,
            decay_rate,
        )
        across = [(0, 2), (1, 3), (2, 0), (3, 1)]
        beside = [(0, 1), (1, 0), (2, 3), (3, 2)]

        def move(value, pairs):
            return lax.ppermute(value, "dp", pairs)

        nbr = [mid] + [move(tails[n], across) for n in range(1, len(tails))]
        par = [move(part, beside) for part in tails]
        fwd = [move(part, beside) for part in nbr]
        mom_new, weight_new, full = publish(mom_new, weight_new, head)
        full = full.reshape((MATS, 4) + block)
        for n, part in enumerate(tails):
            full = fill(full, TAILS[n], part, par[n], nbr[n], fwd[n])
        return (
            mom_new.reshape((MATS,) + block),
            weight_new.reshape((MATS,) + block),
            full.reshape(MATS, ROWS, CB),
        )

    return jax.shard_map(
        local_step,
        mesh=mesh,
        in_specs=(P(("rep", "dp"), None, None, "tp"), P("rep", "dp", "tp"), P("rep", "dp", "tp"), P("rep"), P()),
        out_specs=(P("rep", "dp", "tp"), P("rep", "dp", "tp"), P("rep", None, "tp")),
        check_vma=False,
    )
```

profile of v0, /device:TPU:0, one launch (start us, length us, event | category | flops | bytes accessed | tf_op | source)
XLA Modules:
  0.0 871.7 jit_solution(1500934846153169426)
XLA Ops:
  1.3 759.5 %muon_step.1 = (f32[24,512,384]{2,1,0:T(8,128)}, f32[24,512,384]{2,1,0:T(8,128)}, bf16[16,4,512,384]{3,2,1,0:T(8,128)(2,1)}, bf16[1,512,384]{2,1,0:T(8,128)(2,1)...) custom-call(f32[24,2,2,512,384]{4,3,2,1,0:T(8,128)} %bitcast.grad, ...), custom_call_target="tpu_custom_call" | custom-call | flops 86100000768 | bytes 400000000 | tf_op jit(solution)/shard_map/muon_step/pallas_call | solution.py:567
  760.8 1.5 collective-permute-start.10
  762.3 0.5 collective-permute-start.7
  762.9 0.0 collective-permute-start.12
  762.9 0.5 collective-permute-start.13
  763.4 0.0 collective-permute-start.9
  763.4 1.4 collective-permute-done.12.par
  764.8 0.1 collective-permute-start.6
  764.9 0.4 collective-permute-done.13.fwd
  765.3 1.5 collective-permute-start.4
  766.8 48.3 %collective-permute-done.7.nbr = bf16[2,512,384]{2,1,0:T(8,128)(2,1)S(1)} collective-permute-done((bf16[2,512,384]{2,1,0:T(8,128)(2,1)}, bf16[2,512,384]{2,1,0:T(8,128)(2,1)S(1)}, u32[]{:S(2)}, u32[]{:S(2)}) %collective-permute-start.7) | collective-permute-done | bytes 786464 | tf_op jit(solution)/shard_map/ppermute | solution.py:621
  815.2 0.0 collective-permute-start.8
  815.2 0.0 collective-permute-done.10.nbr
  815.2 0.5 collective-permute-start.11
  815.7 0.0 copy-start.2
  815.7 0.0 copy-start.3
  815.7 43.2 %publish.1 = (f32[12288,384]{1,0:T(8,128)}, f32[12288,384]{1,0:T(8,128)}, bf16[49152,384]{1,0:T(8,128)(2,1)}) custom-call(f32[12288,384]{1,0:T(8,128)} %bitcast.13, f32[12288,384]{1,0:T(8,128)} %bitcast.14, bf16[32768,384]{1,0:T(8,128)(2,1)} %bitcast.10), custom_call_target="tpu_custom_call" | custom-call | flops 40000000000 | bytes 126000000 | tf_op jit(solution)/shard_map/publish/pallas_call | solution.py:507
  858.9 0.0 copy-done.2
  858.9 0.0 copy-done.3
  858.9 0.0 copy-start.5
  858.9 0.0 copy-start.4
  858.9 0.0 copy-start
  858.9 1.2 fill.5.whole
  860.1 0.0 collective-permute-done.4.nbr
  860.1 0.0 copy-done.5
  860.2 0.0 collective-permute-start.3
  860.2 0.0 collective-permute-done.9.par
  860.2 0.0 copy-done.4
  860.2 0.0 copy-start.1
  860.2 1.5 collective-permute-start.1
  861.7 0.0 collective-permute-done.11.fwd
  861.7 0.2 collective-permute-start.5
  861.9 0.0 copy-done
  861.9 2.8 fill.6.whole
  864.7 2.8 collective-permute-done.1.nbr
  867.5 0.0 collective-permute-start
  867.5 0.0 collective-permute-done.6.par
  867.5 0.5 collective-permute-start.2
  868.0 0.0 collective-permute-done.8.fwd
  868.0 0.0 copy-done.1
  868.0 1.7 fill.7.whole
  869.8 0.0 collective-permute-done.3.par
  869.8 0.0 collective-permute-done.5.fwd
  869.8 0.9 fill.8.whole
  870.7 0.0 collective-permute-done.par
  870.7 0.0 collective-permute-done.2.fwd
  870.8 0.9 fill.9
Async XLA Ops:
  760.8 54.4 %collective-permute-start.10 = (bf16[4,512,384]{2,1,0:T(8,128)(2,1)}, bf16[4,512,384]{2,1,0:T(8,128)(2,1)S(1)}, u32[]{:S(2)}, u32[]{:S(2)}) collective-permute-start(bf16[4,512,384]{2,1,0:T(8,128)(2,1)} %get-tuple-element.23.own), channel_id=1, source_target_pairs={{0,2},{1,3},{2,0},{3,1},{4,6},{5,7},{6,4},{7,5}} | collective-permute-start | bytes 4718600 | tf_op jit(solution)/shard_map/ppermute | solution.py:621
  762.3 52.8 %collective-permute-start.7 = (bf16[2,512,384]{2,1,0:T(8,128)(2,1)}, bf16[2,512,384]{2,1,0:T(8,128)(2,1)S(1)}, u32[]{:S(2)}, u32[]{:S(2)}) collective-permute-start(bf16[2,512,384]{2,1,0:T(8,128)(2,1)} %get-tuple-element.22.own), channel_id=1, source_target_pairs={{0,2},{1,3},{2,0},{3,1},{4,6},{5,7},{6,4},{7,5}} | collective-permute-start | bytes 2359304 | tf_op jit(solution)/shard_map/ppermute | solution.py:621
  762.9 1.9 collective-permute-start.12
  762.9 2.5 collective-permute-start.13
  763.4 96.8 %collective-permute-start.9 = (bf16[4,512,384]{2,1,0:T(8,128)(2,1)}, bf16[4,512,384]{2,1,0:T(8,128)(2,1)S(1)}, u32[]{:S(2)}, u32[]{:S(2)}) collective-permute-start(bf16[4,512,384]{2,1,0:T(8,128)(2,1)} %get-tuple-element.23.own), channel_id=1, source_target_pairs={{0,1},{1,0},{2,3},{3,2},{4,5},{5,4},{6,7},{7,6}} | collective-permute-start | bytes 4718600 | tf_op jit(solution)/shard_map/ppermute | solution.py:621
  764.8 102.7 %collective-permute-start.6 = (bf16[2,512,384]{2,1,0:T(8,128)(2,1)}, bf16[2,512,384]{2,1,0:T(8,128)(2,1)S(1)}, u32[]{:S(2)}, u32[]{:S(2)}) collective-permute-start(bf16[2,512,384]{2,1,0:T(8,128)(2,1)} %get-tuple-element.22.own), channel_id=1, source_target_pairs={{0,1},{1,0},{2,3},{3,2},{4,5},{5,4},{6,7},{7,6}} | collective-permute-start | bytes 2359304 | tf_op jit(solution)/shard_map/ppermute | solution.py:621
  765.3 94.8 %collective-permute-start.4 = (bf16[1,256,384]{2,1,0:T(8,128)(2,1)}, bf16[1,256,384]{2,1,0:T(8,128)(2,1)S(1)}, u32[]{:S(2)}, u32[]{:S(2)}) collective-permute-start(bf16[1,256,384]{2,1,0:T(8,128)(2,1)} %get-tuple-element.21.own), channel_id=1, source_target_pairs={{0,2},{1,3},{2,0},{3,1},{4,6},{5,7},{6,4},{7,5}} | collective-permute-start | bytes 589832 | tf_op jit(solution)/shard_map/ppermute | solution.py:621
  815.2 52.9 %collective-permute-start.8 = (bf16[2,512,384]{2,1,0:T(8,128)(2,1)S(1)}, bf16[2,512,384]{2,1,0:T(8,128)(2,1)S(1)}, u32[]{:S(2)}, u32[]{:S(2)}) collective-permute-start(bf16[2,512,384]{2,1,0:T(8,128)(2,1)S(1)} %collective-permute-done.7.nbr), channel_id=1, source_target_pairs={{0,1},{1,0},{2,3},{3,2},{4,5},{5,4},{6,7},{7,6}} | collective-permute-start | bytes 2359304 | tf_op jit(solution)/shard_map/ppermute | solution.py:621
  815.2 46.6 %collective-permute-start.11 = (bf16[4,512,384]{2,1,0:T(8,128)(2,1)S(1)}, bf16[4,512,384]{2,1,0:T(8,128)(2,1)S(1)}, u32[]{:S(2)}, u32[]{:S(2)}) collective-permute-start(bf16[4,512,384]{2,1,0:T(8,128)(2,1)S(1)} %collective-permute-done.10.nbr), channel_id=1, source_target_pairs={{0,1},{1,0},{2,3},{3,2},{4,5},{5,4},{6,7},{7,6}} | collective-permute-start | bytes 4718600 | tf_op jit(solution)/shard_map/ppermute | solution.py:621
  815.7 43.2 %copy-start.2 = (bf16[1,512,384]{2,1,0:T(8,128)(2,1)S(1)}, bf16[1,512,384]{2,1,0:T(8,128)(2,1)}, u32[]{:S(2)}) copy-start(bf16[1,512,384]{2,1,0:T(8,128)(2,1)} %get-tuple-element.24.own) | copy-start | bytes 1179652
  815.7 43.2 %copy-start.3 = (bf16[1,512,384]{2,1,0:T(8,128)(2,1)S(1)}, bf16[1,512,384]{2,1,0:T(8,128)(2,1)}, u32[]{:S(2)}) copy-start(bf16[1,512,384]{2,1,0:T(8,128)(2,1)} %get-tuple-element.25.nbr) | copy-start | bytes 1179652
  858.9 1.2 copy-start.5
  858.9 1.3 copy-start.4
  858.9 3.0 copy-start
  860.2 9.6 %collective-permute-start.3 = (bf16[1,256,384]{2,1,0:T(8,128)(2,1)S(1)}, bf16[1,256,384]{2,1,0:T(8,128)(2,1)S(1)}, u32[]{:S(2)}, u32[]{:S(2)}) collective-permute-start(bf16[1,256,384]{2,1,0:T(8,128)(2,1)S(1)} %copy-done.5), channel_id=1, source_target_pairs={{0,1},{1,0},{2,3},{3,2},{4,5},{5,4},{6,7},{7,6}} | collective-permute-start | bytes 589832 | tf_op jit(solution)/shard_map/ppermute | solution.py:621
  860.2 7.8 copy-start.1
  860.2 7.3 collective-permute-start.1
  861.7 8.1 collective-permute-start.5
  867.5 3.2 collective-permute-start
  867.5 3.2 collective-permute-start.2
where the time goes:
time: 872 us
  Pallas kernels  810 us (93%)
  waiting for transfers between devices  53 us (6%)
    pallas_call x1, Pallas kernels, local_step(): pl.pallas_call(kernel, name='muon_step', out_shape=(jax.ShapeDtypeStruct(...  760 us
    ppermute x14, waiting for transfers between devices, move(): return lax.ppermute(value, 'dp', pairs)  53 us
    pallas_call x1, Pallas kernels, publish(): pl.pallas_call(publish_kernel, name='publish', grid=(steps,), out_shape=(...  43.2 us
  transfers between devices with their start and end apart: 14, of which 4 were waited for; matrix products, arithmetic and copies ran while one was open for 0% of the time, Pallas kernels for 6%

commit v1 on v0

--- a/solution.py
+++ b/solution.py
@@ -39,8 +39,8 @@
 CHUNK = 64
 HEAD = MATS - DEVS
 TAILS = ((0, 1, 0, RB), (1, 4, 0, RB), (5, 2, 0, RB), (7, 1, 0, RB // 2), (7, 1, RB // 2, RB // 2))
-PIECES = 4
-PIECE = RB // PIECES
+PIECES = ((0, 64), (64, 64), (128, 128), (256, 256))
+LAST = len(PIECES)
 
 
 def rem(a, b):
@@ -197,10 +197,10 @@
             a_copy(t + LEAD).start()
 
     def piece_copy(q):
-        if q == PIECES:
+        if q == LAST:
             src, dst = grad.at[0, x, 1 - c], ra.at[0, x]
         else:
-            rows = pl.ds(q * PIECE, PIECE)
+            rows = pl.ds(*PIECES[q])
             src, dst = wtq.at[0, rows, :], ra.at[0, 1 - x, rows, :]
         return remote(src, dst, p_send.at[q], p_recv.at[q], partner)
 
@@ -209,14 +209,23 @@
 
     def presum_first():
         own_copy(0).wait()
-        for q in range(PIECES):
+        for q in range(LAST):
             piece_copy(q).wait_recv()
-            rows = pl.ds(q * PIECE, PIECE)
+            rows = pl.ds(*PIECES[q])
             sendb[0, rows, :] = own[0, 1 - x, rows, :] + ra[0, 1 - x, rows, :]
             remote(
                 sendb.at[0, rows, :], recvb.at[0, rows, :], rs_send.at[0], rs_recv.at[0], nbr
             ).start()
-        piece_copy(PIECES).wait_recv()
+            if q == 0:
+                piece_copy(LAST).start()
+                for t in range(1, LEAD):
+                    a_copy(t).start()
+                own_copy(1).start()
+                rate_copy().start()
+                for t in range(2):
+                    mom_load(t).start()
+                    wt_load(t).start()
+        piece_copy(LAST).wait_recv()
 
         def body(rows):
             acc[0, rows, :] = own[0, x, rows, :] + ra[0, x, rows, :]
@@ -224,7 +233,7 @@
         row_loop(RB, body)
         own_copy(2).start()
         a_copy(LEAD).start()
-        for q in range(PIECES + 1):
+        for q in range(LAST + 1):
             piece_copy(q).wait_send()
 
     def finish(j):
@@ -406,23 +415,17 @@
             forward(w - DEVS)
 
     barrier = pltpu.get_barrier_semaphore()
-    for i in range(1, DEVS):
-        yy, dd = coords(i)
+    beside = dp + 1 - 2 * c
+    peers = [(1 - y, dd) for dd in (3 - dp, nbr_dp, dp, beside)]
+    for yy, dd in peers + [(y, dd) for dd in (3 - dp, nbr_dp, beside)]:
         pl.semaphore_signal(barrier, inc=1, device_id={"tp": yy, "dp": dd}, device_id_type=MESH)
     stage_copy().start()
     own_copy(0).start()
     pl.semaphore_wait(barrier, DEVS - 1)
 
     stage_copy().wait()
-    for q in range(PIECES + 1):
+    for q in range(LAST):
         piece_copy(q).start()
-    for t in range(1, LEAD):
-        a_copy(t).start()
-    own_copy(1).start()
-    rate_copy().start()
-    for t in range(2):
-        mom_load(t).start()
-        wt_load(t).start()
     presum_first()
     rate_copy().wait()
 
@@ -594,7 +597,7 @@
                 pltpu.VMEM((MATS,) + block, BF16),
                 pltpu.VMEM((COLS, COLS), BF16),
                 pltpu.VMEM((COLS, COLS), BF16),
-                dma((1,)), dma((PIECES + 1,)), dma((PIECES + 1,)),
+                dma((1,)), dma((LAST + 1,)), dma((LAST + 1,)),
                 dma((2,)), dma((A_SLOTS,)), dma((A_SLOTS,)), dma((LAG,)), dma((B_SLOTS,)),
                 dma((2,)), dma((2,)), dma((2,)), dma((2,)),
                 dma((DEVS,)), dma((MATS,)), dma((MATS,)), dma((MATS,)),

time: 872 us -> 872 us (level)
  no operation moved by 1% of the time
where the time goes in v1:
time: 872 us
  Pallas kernels  810 us (93%)
  waiting for transfers between devices  53.1 us (6%)
    pallas_call x1, Pallas kernels, local_step(): pl.pallas_call(kernel, name='muon_step', out_shape=(jax.ShapeDtypeStruct(...  759 us
    ppermute x14, waiting for transfers between devices, move(): return lax.ppermute(value, 'dp', pairs)  53.1 us
    pallas_call x1, Pallas kernels, publish(): pl.pallas_call(publish_kernel, name='publish', grid=(steps,), out_shape=(...  43.2 us
  transfers between devices with their start and end apart: 14, of which 4 were waited for; matrix products, arithmetic and copies ran while one was open for 0% of the time, Pallas kernels for 6%

profile of v1, /device:TPU:0, one launch (start us, length us, event | category | flops | bytes accessed | tf_op | source)
XLA Modules:
  0.0 871.5 jit_solution(17364647437257407540)
XLA Ops:
  1.3 759.4 %muon_step.1 = (f32[24,512,384]{2,1,0:T(8,128)}, f32[24,512,384]{2,1,0:T(8,128)}, bf16[16,4,512,384]{3,2,1,0:T(8,128)(2,1)}, bf16[1,512,384]{2,1,0:T(8,128)(2,1)...) custom-call(f32[24,2,2,512,384]{4,3,2,1,0:T(8,128)} %bitcast.grad, ...), custom_call_target="tpu_custom_call" | custom-call | flops 86100000768 | bytes 400000000 | tf_op jit(solution)/shard_map/muon_step/pallas_call | solution.py:570
  760.7 1.5 collective-permute-start.10
  762.1 0.6 collective-permute-start.7
  762.7 0.0 collective-permute-start.12
  762.7 0.5 collective-permute-start.13
  763.2 0.0 collective-permute-start.9
  763.2 1.4 collective-permute-done.12.par
  764.6 0.1 collective-permute-start.6
  764.8 0.4 collective-permute-done.13.fwd
  765.2 1.5 collective-permute-start.4
  766.7 48.3 %collective-permute-done.7.nbr = bf16[2,512,384]{2,1,0:T(8,128)(2,1)S(1)} collective-permute-done((bf16[2,512,384]{2,1,0:T(8,128)(2,1)}, bf16[2,512,384]{2,1,0:T(8,128)(2,1)S(1)}, u32[]{:S(2)}, u32[]{:S(2)}) %collective-permute-start.7) | collective-permute-done | bytes 786464 | tf_op jit(solution)/shard_map/ppermute | solution.py:624
  815.0 0.0 collective-permute-start.8
  815.0 0.0 collective-permute-done.10.nbr
  815.0 0.5 collective-permute-start.11
  815.5 0.0 copy-start.2
  815.5 0.0 copy-start.3
  815.5 43.2 %publish.1 = (f32[12288,384]{1,0:T(8,128)}, f32[12288,384]{1,0:T(8,128)}, bf16[49152,384]{1,0:T(8,128)(2,1)}) custom-call(f32[12288,384]{1,0:T(8,128)} %bitcast.13, f32[12288,384]{1,0:T(8,128)} %bitcast.14, bf16[32768,384]{1,0:T(8,128)(2,1)} %bitcast.10), custom_call_target="tpu_custom_call" | custom-call | flops 40000000000 | bytes 126000000 | tf_op jit(solution)/shard_map/publish/pallas_call | solution.py:510
  858.7 0.0 copy-done.2
  858.7 0.0 copy-done.3
  858.8 0.0 copy-start.5
  858.8 0.0 copy-start.4
  858.8 0.0 copy-start
  858.8 1.2 fill.5.whole
  860.0 0.0 collective-permute-done.4.nbr
  860.0 0.0 copy-done.5
  860.0 0.0 collective-permute-start.3
  860.0 0.0 collective-permute-done.9.par
  860.0 0.0 copy-done.4
  860.1 0.0 copy-start.1
  860.1 1.5 collective-permute-start.1
  861.5 0.0 collective-permute-done.11.fwd
  861.6 0.2 collective-permute-start.5
  861.7 0.0 copy-done
  861.7 2.8 fill.6.whole
  864.5 2.8 collective-permute-done.1.nbr
  867.4 0.0 collective-permute-start
  867.4 0.0 collective-permute-done.6.par
  867.4 0.5 collective-permute-start.2
  867.9 0.0 collective-permute-done.8.fwd
  867.9 0.0 copy-done.1
  867.9 1.7 fill.7.whole
  869.6 0.0 collective-permute-done.3.par
  869.6 0.0 collective-permute-done.5.fwd
  869.6 0.9 fill.8.whole
  870.6 0.0 collective-permute-done.par
  870.6 0.0 collective-permute-done.2.fwd
  870.6 0.9 fill.9
Async XLA Ops:
  760.7 54.4 %collective-permute-start.10 = (bf16[4,512,384]{2,1,0:T(8,128)(2,1)}, bf16[4,512,384]{2,1,0:T(8,128)(2,1)S(1)}, u32[]{:S(2)}, u32[]{:S(2)}) collective-permute-start(bf16[4,512,384]{2,1,0:T(8,128)(2,1)} %get-tuple-element.23.own), channel_id=1, source_target_pairs={{0,2},{1,3},{2,0},{3,1},{4,6},{5,7},{6,4},{7,5}} | collective-permute-start | bytes 4718600 | tf_op jit(solution)/shard_map/ppermute | solution.py:624
  762.1 52.9 %collective-permute-start.7 = (bf16[2,512,384]{2,1,0:T(8,128)(2,1)}, bf16[2,512,384]{2,1,0:T(8,128)(2,1)S(1)}, u32[]{:S(2)}, u32[]{:S(2)}) collective-permute-start(bf16[2,512,384]{2,1,0:T(8,128)(2,1)} %get-tuple-element.22.own), channel_id=1, source_target_pairs={{0,2},{1,3},{2,0},{3,1},{4,6},{5,7},{6,4},{7,5}} | collective-permute-start | bytes 2359304 | tf_op jit(solution)/shard_map/ppermute | solution.py:624
  762.7 1.9 collective-permute-start.12
  762.7 2.5 collective-permute-start.13
  763.2 96.8 %collective-permute-start.9 = (bf16[4,512,384]{2,1,0:T(8,128)(2,1)}, bf16[4,512,384]{2,1,0:T(8,128)(2,1)S(1)}, u32[]{:S(2)}, u32[]{:S(2)}) collective-permute-start(bf16[4,512,384]{2,1,0:T(8,128)(2,1)} %get-tuple-element.23.own), channel_id=1, source_target_pairs={{0,1},{1,0},{2,3},{3,2},{4,5},{5,4},{6,7},{7,6}} | collective-permute-start | bytes 4718600 | tf_op jit(solution)/shard_map/ppermute | solution.py:624
  764.6 102.7 %collective-permute-start.6 = (bf16[2,512,384]{2,1,0:T(8,128)(2,1)}, bf16[2,512,384]{2,1,0:T(8,128)(2,1)S(1)}, u32[]{:S(2)}, u32[]{:S(2)}) collective-permute-start(bf16[2,512,384]{2,1,0:T(8,128)(2,1)} %get-tuple-element.22.own), channel_id=1, source_target_pairs={{0,1},{1,0},{2,3},{3,2},{4,5},{5,4},{6,7},{7,6}} | collective-permute-start | bytes 2359304 | tf_op jit(solution)/shard_map/ppermute | solution.py:624
  765.2 94.8 %collective-permute-start.4 = (bf16[1,256,384]{2,1,0:T(8,128)(2,1)}, bf16[1,256,384]{2,1,0:T(8,128)(2,1)S(1)}, u32[]{:S(2)}, u32[]{:S(2)}) collective-permute-start(bf16[1,256,384]{2,1,0:T(8,128)(2,1)} %get-tuple-element.21.own), channel_id=1, source_target_pairs={{0,2},{1,3},{2,0},{3,1},{4,6},{5,7},{6,4},{7,5}} | collective-permute-start | bytes 589832 | tf_op jit(solution)/shard_map/ppermute | solution.py:624
  815.0 52.9 %collective-permute-start.8 = (bf16[2,512,384]{2,1,0:T(8,128)(2,1)S(1)}, bf16[2,512,384]{2,1,0:T(8,128)(2,1)S(1)}, u32[]{:S(2)}, u32[]{:S(2)}) collective-permute-start(bf16[2,512,384]{2,1,0:T(8,128)(2,1)S(1)} %collective-permute-done.7.nbr), channel_id=1, source_target_pairs={{0,1},{1,0},{2,3},{3,2},{4,5},{5,4},{6,7},{7,6}} | collective-permute-start | bytes 2359304 | tf_op jit(solution)/shard_map/ppermute | solution.py:624
  815.0 46.5 %collective-permute-start.11 = (bf16[4,512,384]{2,1,0:T(8,128)(2,1)S(1)}, bf16[4,512,384]{2,1,0:T(8,128)(2,1)S(1)}, u32[]{:S(2)}, u32[]{:S(2)}) collective-permute-start(bf16[4,512,384]{2,1,0:T(8,128)(2,1)S(1)} %collective-permute-done.10.nbr), channel_id=1, source_target_pairs={{0,1},{1,0},{2,3},{3,2},{4,5},{5,4},{6,7},{7,6}} | collective-permute-start | bytes 4718600 | tf_op jit(solution)/shard_map/ppermute | solution.py:624
  815.5 43.2 %copy-start.2 = (bf16[1,512,384]{2,1,0:T(8,128)(2,1)S(1)}, bf16[1,512,384]{2,1,0:T(8,128)(2,1)}, u32[]{:S(2)}) copy-start(bf16[1,512,384]{2,1,0:T(8,128)(2,1)} %get-tuple-element.24.own) | copy-start | bytes 1179652
  815.5 43.2 %copy-start.3 = (bf16[1,512,384]{2,1,0:T(8,128)(2,1)S(1)}, bf16[1,512,384]{2,1,0:T(8,128)(2,1)}, u32[]{:S(2)}) copy-start(bf16[1,512,384]{2,1,0:T(8,128)(2,1)} %get-tuple-element.25.nbr) | copy-start | bytes 1179652
  858.8 1.2 copy-start.5
  858.8 1.3 copy-start.4
  858.8 3.0 copy-start
  860.0 9.6 %collective-permute-start.3 = (bf16[1,256,384]{2,1,0:T(8,128)(2,1)S(1)}, bf16[1,256,384]{2,1,0:T(8,128)(2,1)S(1)}, u32[]{:S(2)}, u32[]{:S(2)}) collective-permute-start(bf16[1,256,384]{2,1,0:T(8,128)(2,1)S(1)} %copy-done.5), channel_id=1, source_target_pairs={{0,1},{1,0},{2,3},{3,2},{4,5},{5,4},{6,7},{7,6}} | collective-permute-start | bytes 589832 | tf_op jit(solution)/shard_map/ppermute | solution.py:624
  860.1 7.8 copy-start.1
  860.1 7.3 collective-permute-start.1
  861.6 8.1 collective-permute-start.5
  867.4 3.2 collective-permute-start
  867.4 3.2 collective-permute-start.2
